TPU v7x, 256 devices: a whole 4x4x8 slice. The times are simulated.
256 devices in a mesh: dp: 16 (over y, x_hi, core), space: 16 (over x_lo, z).
Axes of the slice: x: 4 (x_hi: 2, x_lo: 2; x = x_hi * 2 + x_lo), y: 4, z: 8, core: 2. Of those that a mesh axis runs over, the one named last changes fastest.
Arguments:
- act_in: bfloat16 [16, 32, 64, 2048], P('dp', 'space'), may hold values from -6 to 6
- weight_one: bfloat16 [3, 3, 3, 32, 64], replicated, may hold values from -0.21875 to 0.21875
- bias_one: float32 [64], replicated, may hold values from -3 to 3
- weight_two: bfloat16 [3, 3, 3, 64, 128], replicated, may hold values from -0.15625 to 0.15625
- bias_two: float32 [128], replicated, may hold values from -3 to 3
- cotangent: bfloat16 [16, 16, 32, 4096], P('dp', 'space'), may hold values from -24 to 24
Outputs:
- grad_input: bfloat16 [16, 32, 64, 2048], P('dp', 'space')
- grad_w_one: float32 [3, 3, 3, 32, 64], replicated
- grad_b_one: float32 [64], replicated
- grad_w_two: float32 [3, 3, 3, 64, 128], replicated
- grad_b_two: float32 [128], replicated
All inputs are finite; a program needn't handle non-finite values.
Results may differ from a plain program's by a relative error of at most 0.01.
Values may be sent and summed in bfloat16 or wider, within the bound.
No kernel may reach another device: no remote copies, remote signals or barrier semaphores. Data moves between devices by JAX's collectives and lax.ppermute only.
A program may use at most 128 MiB of HBM per device.

v0:
```python
import math
import jax
import jax.numpy as jnp
from jax import lax
from jax.sharding import PartitionSpec as P


def padded_2(cells, sides, width):
    for axis, dim in sides:
        count = lax.axis_size(axis)
        ends = count - 1
        head = lax.slice_in_dim(cells, 0, width, axis=dim)
        tail = lax.slice_in_dim(cells, cells.shape[dim] - width, cells.shape[dim], axis=dim)
        cells = jnp.concatenate(
            [
                lax.ppermute(tail, axis, [(i, (i + 1) % count) for i in range(ends)]),
                cells,
                lax.ppermute(head, axis, [((i + 1) % count, i) for i in range(ends)]),
            ],
            axis=dim,
        )
    return cells


def forward_conv(padded, kernel):
    return lax.conv_general_dilated(
        padded,
        kernel,
        (1, 1, 1),
        ((0, 0), (1, 1), (1, 1)),
        dimension_numbers=("NDHWC", "DHWIO", "NDHWC"),
        preferred_element_type=jnp.float32,
    )


def weight_grad(padded, delta):
    return lax.conv_general_dilated(
        padded,
        delta,
        (1, 1, 1),
        ((0, 0), (1, 1), (1, 1)),
        dimension_numbers=("CDHWN", "IDHWO", "DHWNC"),
        preferred_element_type=jnp.float32,
    )


def input_grad(delta, kernel, depth_pad):
    return lax.conv_general_dilated(
        delta,
        kernel[::-1, ::-1, ::-1],
        (1, 1, 1),
        (depth_pad, (1, 1), (1, 1)),
        dimension_numbers=("NDHWC", "DHWOI", "NDHWC"),
        preferred_element_type=jnp.float32,
    )


def silu_slope(value):
    sig = jax.nn.sigmoid(value)
    return sig * (1.0 + value * (1.0 - sig))


def local(act_in, weight_one, bias_one, weight_two, bias_two, cotangent):
    samples, slab, side, merged = act_in.shape
    chan_in = weight_one.shape[3]
    chan_mid = weight_one.shape[4]
    chan_out = weight_two.shape[4]
    half = side // 2
    slab_two = slab // 2
    batch_all = samples * lax.axis_size("dp")
    depth_all = slab * lax.axis_size("space")
    scale_one = 16.0 / math.sqrt(batch_all * depth_all * side * side)
    scale_two = 1.0 / math.sqrt(batch_all * (depth_all // 2) * half * half)
    x_pad = padded_2(act_in, (("space", 1),), 1).reshape(samples, slab + 2, side, side, chan_in)
    pre_one = forward_conv(x_pad, weight_one) + bias_one
    act_one = pre_one * jax.nn.sigmoid(pre_one)
    pooled = (
        act_one.reshape(samples, slab_two, 2, half, 2, half, 2, chan_mid)
        .mean(axis=(2, 4, 6))
        .astype(jnp.bfloat16)
    )
    pool_pad = padded_2(
        pooled.reshape(samples, slab_two, half, half * chan_mid), (("space", 1),), 1
    ).reshape(samples, slab_two + 2, half, half, chan_mid)
    pre_two = forward_conv(pool_pad, weight_two) + bias_two
    cot_five = cotangent.reshape(samples, slab_two, half, half, chan_out)
    delta_two = (cot_five.astype(jnp.float32) * silu_slope(pre_two)).astype(jnp.bfloat16)
    gw_two = weight_grad(pool_pad, delta_two)
    gb_two = jnp.sum(delta_two, axis=(0, 1, 2, 3), dtype=jnp.float32)
    gw_two, gb_two = lax.psum((gw_two, gb_two), ("dp", "space"))
    delta_pad = padded_2(
        delta_two.reshape(samples, slab_two, half, half * chan_out), (("space", 1),), 1
    ).reshape(samples, slab_two + 2, half, half, chan_out)
    grad_pooled = input_grad(delta_pad, weight_two, (0, 0))
    spread = jnp.broadcast_to(
        grad_pooled[:, :, None, :, None, :, None, :],
        (samples, slab_two, 2, half, 2, half, 2, chan_mid),
    ).reshape(samples, slab, side, side, chan_mid)
    delta_one = (spread / 8.0 * silu_slope(pre_one)).astype(jnp.bfloat16)
    gw_one = weight_grad(x_pad, delta_one)
    gb_one = jnp.sum(delta_one, axis=(0, 1, 2, 3), dtype=jnp.float32)
    delta_one_pad = padded_2(
        delta_one.reshape(samples, slab, side, side * chan_mid), (("space", 1),), 1
    ).reshape(samples, slab + 2, side, side, chan_mid)
    grad_x = input_grad(delta_one_pad, weight_one, (0, 0))
    gw_one, gb_one = lax.psum((gw_one, gb_one), ("dp", "space"))
    grad_input = grad_x.astype(jnp.bfloat16).reshape(samples, slab, side, side * chan_in)
    return (
        grad_input,
        gw_one * scale_one,
        gb_one * scale_one,
        gw_two * scale_two,
        gb_two * scale_two,
    )


def solution(mesh):
    placed = (P("dp", "space", None, None), P(), P(), P(), P(), P("dp", "space", None, None))
    return jax.shard_map(
        local,
        mesh=mesh,
        in_specs=placed,
        out_specs=(P("dp", "space", None, None), P(), P(), P(), P()),
        check_vma=False,
    )
```

profile of v0, /device:TPU:1, one launch (start us, length us, event | category | flops | bytes accessed | tf_op | source)
XLA Modules:
  0.0 471.9 jit_solution(11770701972416479829)
XLA Ops:
  8.9 4.4 collective-permute-start
  14.6 9.3 %collective-permute-done = bf16[1,1,64,2048]{2,3,1,0:T(8,128)(2,1)S(1)} collective-permute-done((bf16[1,1,64,2048]{2,3,1,0:T(8,128)(2,1)S(1)}, bf16[1,1,64,2048]{2,3,1,0:T(8,128)(2,1)S(1)}, u32[]{:S(2)}, u32[]{:S(2)}) %collective-permute-start) | collective-permute-done | bytes 262176 | tf_op jit(solution)/shard_map/ppermute | solution.py:16
  23.8 4.2 collective-permute-done.1
  31.7 6.7 %copy.179 = bf16[4,64,1,8,9,32]{5,3,4,1,0,2:T(8,128)(2,1)} copy(bf16[4,64,1,8,9,32]{1,5,4,3,0,2:T(8,128)(2,1)} %bitcast.114) | data formatting | bytes 2359296 | tf_op jit(solution)/shard_map/conv_general_dilated | solution.py:26
  40.0 11.3 %fusion.16 = (f32[2,64,8,9,64]{4,2,3,1,0:T(8,128)S(1)}, f32[2,64,8,9,64]{4,2,3,1,0:T(8,128)}) fusion(f32[64]{0:T(128)S(1)} %copy-done.9, pred[8,9]{0,1:T(8,128)(4,1)S(1)} %copy-done.11, bf16[3,3,3,32,64]{4,3,2,1,0:T(8,128)(2,1)S(1)} %copy-done.7, bf16[4,64,1,7,2,32]{5,3,4,1,0,2:T(8,128)(2,1)S(1)} %slice.27, bf16[4,64,1,8,9,32]{5,3,4,1,0,2:T(8,128)(2,1)} %copy.179), kind=kOutput, calls=%fused_computation.18 | convolution fusion | flops 1018822656 | bytes 6238536 | tf_op jit(solution)/shard_map/conv_general_dilated | solution.py:26
  54.2 3.3 reduce_sum.36
  57.9 4.2 collective-permute-start.2
  63.8 5.5 %copy.198 = f32[2,64,8,9,64]{4,1,3,2,0:T(8,128)} copy(f32[2,64,8,9,64]{4,2,3,1,0:T(8,128)} %get-tuple-element.42) | data formatting | bytes 4718592 | tf_op jit(solution)/shard_map/mul | solution.py:60
  69.3 13.0 %copy.205 = bf16[1,4,64,64,32]{4,0,3,2,1:T(2,128)(2,1)} copy(bf16[1,4,64,64,32]{2,4,3,1,0:T(8,128)(2,1)S(1)} %bitcast.106) | data formatting | bytes 2097152 | tf_op jit(solution)/shard_map/reshape | solution.py:74
  90.8 4.9 %collective-permute-start.4 = (bf16[1,1,32,4096]{3,2,1,0:T(8,128)(2,1)S(1)}, bf16[1,1,32,4096]{3,2,1,0:T(8,128)(2,1)S(1)}, u32[]{:S(2)}, u32[]{:S(2)}) collective-permute-start(bf16[1,1,32,4096]{3,2,1,0:T(8,128)(2,1)S(1)} %reshape.106), channel_id=1, source_target_pairs={{0,1},{1,2},{2,3},{3,4},{4,5},{5,6},{6,7},{7,8},{8,9},{9,10},{10,1... | collective-permute-start | bytes 786440 | tf_op jit(solution)/shard_map/ppermute | solution.py:16
  97.4 8.1 %fusion.56 = f32[3,3,3,64,128]{4,3,2,1,0:T(8,128)} fusion(bf16[1,3,32,32,64]{4,0,3,2,1:T(2,128)(2,1)S(1)} %constant_dynamic-update-slice_fusion, bf16[1,1,32,32,128]{4,3,1,2,0:T(8,128)(2,1)S(1)} %get-tuple-element.40), kind=kOutput, calls=%fused_computation.65 | convolution fusion | flops 434307072 | bytes 1540096 | tf_op jit(solution)/shard_map/conv_general_dilated | solution.py:37
  106.6 2.5 fusion.47
  114.0 2.5 reshape.107
  118.8 5.7 %collective-permute-start.6 = (bf16[1,1,64,4096]{3,2,1,0:T(8,128)(2,1)}, bf16[1,1,64,4096]{3,2,1,0:T(8,128)(2,1)}, u32[]{:S(2)}, u32[]{:S(2)}) collective-permute-start(bf16[1,1,64,4096]{3,2,1,0:T(8,128)(2,1)} %get-tuple-element.45), channel_id=1, source_target_pairs={{0,1},{1,2},{2,3},{3,4},{4,5},{5,6},{6,7},{7,8},{8,9},{9,10},{10,1... | collective-permute-start | bytes 1572872 | tf_op jit(solution)/shard_map/ppermute | solution.py:16
  125.8 66.2 %fusion.18 = f32[3,3,3,32,64]{4,3,2,1,0:T(8,128)} fusion(bf16[1,4,64,64,32]{4,0,3,2,1:T(2,128)(2,1)} %copy.205, bf16[1,2,64,64,64]{4,3,2,1,0:T(8,128)(2,1)S(1)} %bitcast.108), kind=kOutput, calls=%fused_computation.25 | convolution fusion | flops 887193600 | bytes 2318336 | tf_op jit(solution)/shard_map/conv_general_dilated | solution.py:37
  192.0 2.8 convert_reduce_fusion
  194.8 83.0 %all-reduce = (f32[64]{0:T(128)S(1)}, f32[128]{0:T(128)S(1)}) all-reduce(f32[64]{0:T(128)S(1)} %convert_reduce_fusion, f32[128]{0:T(128)S(1)} %copy-done.6), channel_id=1, replica_groups=mesh['dp'=16,'space'=16] {'dp','space'}, use_global_device_ids=true, to_apply=%region_4.0 | all-reduce | flops 192 | bytes 1536 | tf_op jit(solution)/shard_map/psum | solution.py:106
  278.9 2.8 concatenate.34
  281.7 2.8 concatenate.35
  286.7 2.7 copy.213
  290.7 3.0 copy.203
  294.0 18.1 %fusion.4 = bf16[2,64,8,9,32]{4,2,3,1,0:T(8,128)(2,1)} fusion(bf16[3,3,3,32,64]{4,3,2,1,0:T(8,128)(2,1)S(1)} %copy-done.8, bf16[4,64,1,7,2,64]{5,3,4,1,0,2:T(8,128)(2,1)S(1)} %slice.36, bf16[4,64,1,8,9,64]{5,3,4,1,0,2:T(8,128)(2,1)S(1)} %copy.203), kind=kOutput, calls=%fused_computation.6 | convolution fusion | flops 1017249792 | bytes 3518464 | tf_op jit(solution)/shard_map/conv_general_dilated | solution.py:48
  312.1 3.2 copy.204
  316.9 143.7 %all-reduce.4.cloned.1.call-done = (f32[3,3,3,32,64]{4,3,2,1,0:T(8,128)}, f32[3,3,3,64,128]{4,3,2,1,0:T(8,128)}) async-done(((f32[3,3,3,32,64]{4,3,2,1,0:T(8,128)}, f32[3,3,3,64,128]{4,3,2,1,0:T(8,128)}), (f32[3,3,3,32,64]{4,3,2,1,0:T(8,128)}, f32[3,3,3,64,128]{4,3,2,1,0:T(8,128)})) %all-reduce.4.cloned.1.call-update) | async-done | bytes 1105936 | tf_op jit(solution)/shard_map/psum | solution.py:106
  (92 shorter events, 43.0 us)
Async XLA Ops:
  7.2 81.0 %copy-start = (bf16[3,3,3,64,128]{4,3,2,1,0:T(8,128)(2,1)S(1)}, bf16[3,3,3,64,128]{4,3,2,1,0:T(8,128)(2,1)}, u32[]{:S(2)}) copy-start(bf16[3,3,3,64,128]{4,3,2,1,0:T(8,128)(2,1)} %param.9) | copy-start | bytes 1327108
  7.2 453.4 %all-reduce.4.cloned.1.call-start = ((), (), s32[]{:S(2)}) async-start(), calls=%async_computation | async-start | bytes 2654208 | tf_op jit(solution)/shard_map/psum | solution.py:106
  8.8 15.0 %copy-start.3 = (bf16[1,2,64,2048]{2,3,1,0:T(8,128)(2,1)}, bf16[1,2,64,2048]{2,3,1,0:T(8,128)(2,1)S(1)}, u32[]{:S(2)}) copy-start(bf16[1,2,64,2048]{2,3,1,0:T(8,128)(2,1)S(1)} %copy.175) | copy-start | bytes 1572868
  8.9 15.0 %collective-permute-start = (bf16[1,1,64,2048]{2,3,1,0:T(8,128)(2,1)S(1)}, bf16[1,1,64,2048]{2,3,1,0:T(8,128)(2,1)S(1)}, u32[]{:S(2)}, u32[]{:S(2)}) collective-permute-start(bf16[1,1,64,2048]{2,3,1,0:T(8,128)(2,1)S(1)} %get-tuple-element.47), channel_id=1, source_target_pairs={{0,1},{1,2},{2,3},{3,4},{4,5},{5,6},{6,7},{7,8},{8,9},{9,10},{10,1... | collective-permute-start | bytes 786440 | tf_op jit(solution)/shard_map/ppermute | solution.py:16
  13.3 14.7 %collective-permute-start.1 = (bf16[1,1,64,2048]{2,3,1,0:T(8,128)(2,1)S(1)}, bf16[1,1,64,2048]{2,3,1,0:T(8,128)(2,1)S(1)}, u32[]{:S(2)}, u32[]{:S(2)}) collective-permute-start(bf16[1,1,64,2048]{2,3,1,0:T(8,128)(2,1)S(1)} %get-tuple-element.48), channel_id=1, source_target_pairs={{1,0},{2,1},{3,2},{4,3},{5,4},{6,5},{7,6},{8,7},{9,8},{10,9},{11,1... | collective-permute-start | bytes 786440 | tf_op jit(solution)/shard_map/ppermute | solution.py:18
  31.7 8.3 %copy-start.7 = (bf16[3,3,3,32,64]{4,3,2,1,0:T(8,128)(2,1)S(1)}, bf16[3,3,3,32,64]{4,3,2,1,0:T(8,128)(2,1)}, u32[]{:S(2)}) copy-start(bf16[3,3,3,32,64]{4,3,2,1,0:T(8,128)(2,1)} %param.7) | copy-start | bytes 331780
  31.7 8.3 %copy-start.9 = (f32[64]{0:T(128)S(1)}, f32[64]{0:T(128)}, u32[]{:S(2)}) copy-start(f32[64]{0:T(128)} %param.8) | copy-start | bytes 772
  31.7 8.3 %copy-start.11 = (pred[8,9]{0,1:T(8,128)(4,1)S(1)}, pred[8,9]{0,1:T(8,128)(4,1)}, u32[]{:S(2)}) copy-start(pred[8,9]{0,1:T(8,128)(4,1)} %constant.38) | copy-start | bytes 220
  52.2 10.0 %copy-start.4 = (bf16[1,1,32,4096]{3,2,1,0:T(8,128)(2,1)S(1)}, bf16[1,1,32,4096]{3,2,1,0:T(8,128)(2,1)}, u32[]{:S(2)}) copy-start(bf16[1,1,32,4096]{3,2,1,0:T(8,128)(2,1)} %param.11) | copy-start | bytes 786436
  57.9 24.4 %collective-permute-start.2 = (bf16[1,1,32,2048]{3,2,1,0:T(8,128)(2,1)S(1)}, bf16[1,1,32,2048]{3,2,1,0:T(8,128)(2,1)}, u32[]{:S(2)}, u32[]{:S(2)}) collective-permute-start(bf16[1,1,32,2048]{3,2,1,0:T(8,128)(2,1)S(1)} %convert_element_type.57), channel_id=1, source_target_pairs={{0,1},{1,2},{2,3},{3,4},{4,5},{5,6},{6,7},{7,8},{8,9},{9,10},{10,1... | collective-permute-start | bytes 393224 | tf_op jit(solution)/shard_map/ppermute | solution.py:16
  62.3 22.4 %collective-permute-start.3 = (bf16[1,1,32,2048]{3,2,1,0:T(8,128)(2,1)S(1)}, bf16[1,1,32,2048]{3,2,1,0:T(8,128)(2,1)}, u32[]{:S(2)}, u32[]{:S(2)}) collective-permute-start(bf16[1,1,32,2048]{3,2,1,0:T(8,128)(2,1)S(1)} %convert_element_type.57), channel_id=1, source_target_pairs={{1,0},{2,1},{3,2},{4,3},{5,4},{6,5},{7,6},{8,7},{9,8},{10,9},{11,1... | collective-permute-start | bytes 393224 | tf_op jit(solution)/shard_map/ppermute | solution.py:18
  84.7 3.5 copy-start.10
  84.7 3.5 copy-start.12
  90.8 14.6 %collective-permute-start.4 = (bf16[1,1,32,4096]{3,2,1,0:T(8,128)(2,1)S(1)}, bf16[1,1,32,4096]{3,2,1,0:T(8,128)(2,1)S(1)}, u32[]{:S(2)}, u32[]{:S(2)}) collective-permute-start(bf16[1,1,32,4096]{3,2,1,0:T(8,128)(2,1)S(1)} %reshape.106), channel_id=1, source_target_pairs={{0,1},{1,2},{2,3},{3,4},{4,5},{5,6},{6,7},{7,8},{8,9},{9,10},{10,1... | collective-permute-start | bytes 786440 | tf_op jit(solution)/shard_map/ppermute | solution.py:16
  95.7 9.8 %collective-permute-start.5 = (bf16[1,1,32,4096]{3,2,1,0:T(8,128)(2,1)S(1)}, bf16[1,1,32,4096]{3,2,1,0:T(8,128)(2,1)S(1)}, u32[]{:S(2)}, u32[]{:S(2)}) collective-permute-start(bf16[1,1,32,4096]{3,2,1,0:T(8,128)(2,1)S(1)} %reshape.106), channel_id=1, source_target_pairs={{1,0},{2,1},{3,2},{4,3},{5,4},{6,5},{7,6},{8,7},{9,8},{10,9},{11,1... | collective-permute-start | bytes 786440 | tf_op jit(solution)/shard_map/ppermute | solution.py:18
  106.5 3.8 slice-start
  106.6 3.7 slice-start.1
  111.1 1.4 copy-start.2
  118.8 160.1 %collective-permute-start.6 = (bf16[1,1,64,4096]{3,2,1,0:T(8,128)(2,1)}, bf16[1,1,64,4096]{3,2,1,0:T(8,128)(2,1)}, u32[]{:S(2)}, u32[]{:S(2)}) collective-permute-start(bf16[1,1,64,4096]{3,2,1,0:T(8,128)(2,1)} %get-tuple-element.45), channel_id=1, source_target_pairs={{0,1},{1,2},{2,3},{3,4},{4,5},{5,6},{6,7},{7,8},{8,9},{9,10},{10,1... | collective-permute-start | bytes 1572872 | tf_op jit(solution)/shard_map/ppermute | solution.py:16
  124.5 157.2 %collective-permute-start.7 = (bf16[1,1,64,4096]{3,2,1,0:T(8,128)(2,1)}, bf16[1,1,64,4096]{3,2,1,0:T(8,128)(2,1)}, u32[]{:S(2)}, u32[]{:S(2)}) collective-permute-start(bf16[1,1,64,4096]{3,2,1,0:T(8,128)(2,1)} %get-tuple-element.46), channel_id=1, source_target_pairs={{1,0},{2,1},{3,2},{4,3},{5,4},{6,5},{7,6},{8,7},{9,8},{10,9},{11,1... | collective-permute-start | bytes 1572872 | tf_op jit(solution)/shard_map/ppermute | solution.py:18
  125.7 69.1 %copy-start.6 = (f32[128]{0:T(128)S(1)}, f32[128]{0:T(128)}, u32[]{:S(2)}) copy-start(f32[128]{0:T(128)} %get-tuple-element.39) | copy-start | bytes 1540
  290.7 3.3 copy-start.8
  294.0 21.3 %copy-start.5 = (pred[8,9]{1,0:T(8,128)(4,1)S(1)}, pred[8,9]{1,0:T(8,128)(4,1)}, u32[]{:S(2)}) copy-start(pred[8,9]{1,0:T(8,128)(4,1)} %constant.34) | copy-start | bytes 220
  312.1 152.5 %copy-start.1 = (bf16[3,3,3,64,128]{4,3,2,1,0:T(8,128)(2,1)S(1)}, bf16[3,3,3,64,128]{4,3,2,1,0:T(8,128)(2,1)}, u32[]{:S(2)}) copy-start(bf16[3,3,3,64,128]{4,3,2,1,0:T(8,128)(2,1)} %param.9) | copy-start | bytes 1327108
Sparse Core Ops, SparseCore 0:
  194.9 265.5 all-reduce.3
where the time goes:
time: 481 us; the launch traced here: 472 us
  waiting for transfers between devices  157 us (33%)
  matrix products  108 us (22%)
  blocking collectives  83 us (17%)
  local copies, waits for them, and re-layouts  64.9 us (13%)
  starting transfers between devices  25 us (5%)
  other arithmetic  19.1 us (4%)
  between operations  15 us (3%)
    psum x1, waiting for transfers between devices, local(): gw_one, gb_one = lax.psum((gw_one, gb_one), ('dp', 'space'))  144 us
    psum x1, blocking collectives, local(): gw_one, gb_one = lax.psum((gw_one, gb_one), ('dp', 'space'))  83 us
    conv_general_dilated x2, matrix products, weight_grad(): lax.conv_general_dilated(padded, delta, (1, 1, 1), ((0, 0), (1, 1), (1, 1...  74.3 us
    conv_general_dilated x2, matrix products, input_grad(): lax.conv_general_dilated(delta, kernel[::-1, ::-1, ::-1], (1, 1, 1), (dep...  20.6 us
    ppermute x4, starting transfers between devices, padded_2(): lax.ppermute(tail, axis, [(i, (i + 1) % count) for i in range(ends)])  19.2 us
    reshape x2, local copies, waits for them, and re-layouts, local(): padded_2(act_in, (('space', 1),), 1)  15 us
    conv_general_dilated x2, matrix products, forward_conv(): lax.conv_general_dilated(padded, kernel, (1, 1, 1), ((0, 0), (1, 1), (1,...  12.8 us
    concatenate x8, local copies, waits for them, and re-layouts, padded_2(): jnp.concatenate([lax.ppermute(tail, axis, [(i, (i + 1) % count) for i in...  10.2 us
  transfers between devices with their start and end apart: 9, of which 3 were waited for; matrix products, arithmetic and copies ran while one was open for 29% of the time, Pallas kernels for 0%

commit v1 on v0

--- a/solution.py
+++ b/solution.py
@@ -103,7 +103,7 @@
         delta_one.reshape(samples, slab, side, side * chan_mid), (("space", 1),), 1
     ).reshape(samples, slab + 2, side, side, chan_mid)
     grad_x = input_grad(delta_one_pad, weight_one, (0, 0))
-    gw_one, gb_one = lax.psum((gw_one, gb_one), ("dp", "space"))
+    gw_one, gb_one = lax.psum(lax.psum((gw_one, gb_one), "space"), "dp")
     grad_input = grad_x.astype(jnp.bfloat16).reshape(samples, slab, side, side * chan_in)
     return (
         grad_input,

time: 481 us -> 865 us (1.80)
  waiting for transfers between devices: 157 us -> 459 us
  blocking collectives: 83 us -> 152 us
  matrix products: 108 us -> 125 us
    psum x1 -> x3, waiting for transfers between devices: 144 us -> 445 us  [the longest x1 269 us: local(): gw_two, gb_two = lax.psum((gw_two, gb_two), ('dp', 'space'))]
    psum x1 -> x3, blocking collectives: 83 us -> 152 us  [the longest x1 82.1 us: local(): gw_two, gb_two = lax.psum((gw_two, gb_two), ('dp', 'space'))]
    conv_general_dilated x2, matrix products: 74.3 us -> 91.8 us  [weight_grad(): lax.conv_general_dilated(padded, delta, (1, 1, 1), ((0, 0), (1, 1), (1, 1...]
  transfers between devices with their start and end apart: 9 -> 11, of which waited for: 3 -> 5; matrix products, arithmetic and copies ran while one was open for 29% -> 5% of each run, Pallas kernels for 0% -> 0%
where the time goes in v1:
time: 865 us; the launch traced here: 857 us
  waiting for transfers between devices  459 us (53%)
  blocking collectives  152 us (18%)
  matrix products  125 us (14%)
  local copies, waits for them, and re-layouts  63.9 us (7%)
  starting transfers between devices  23.9 us (3%)
  other arithmetic  18.7 us (2%)
  between operations  14.6 us (2%)
    psum x1, waiting for transfers between devices, local(): gw_two, gb_two = lax.psum((gw_two, gb_two), ('dp', 'space'))  269 us
    psum x2, waiting for transfers between devices, local(): gw_one, gb_one = lax.psum(lax.psum((gw_one, gb_one), 'space'), 'dp')  177 us
    conv_general_dilated x2, matrix products, weight_grad(): lax.conv_general_dilated(padded, delta, (1, 1, 1), ((0, 0), (1, 1), (1, 1...  91.8 us
    psum x1, blocking collectives, local(): gw_two, gb_two = lax.psum((gw_two, gb_two), ('dp', 'space'))  82.1 us
    psum x2, blocking collectives, local(): gw_one, gb_one = lax.psum(lax.psum((gw_one, gb_one), 'space'), 'dp')  69.5 us
    conv_general_dilated x2, matrix products, input_grad(): lax.conv_general_dilated(delta, kernel[::-1, ::-1, ::-1], (1, 1, 1), (dep...  20.5 us
    ppermute x4, starting transfers between devices, padded_2(): lax.ppermute(tail, axis, [(i, (i + 1) % count) for i in range(ends)])  18 us
  transfers between devices with their start and end apart: 11, of which 5 were waited for; matrix products, arithmetic and copies ran while one was open for 5% of the time, Pallas kernels for 0%

profile of v1, /device:TPU:1, one launch (start us, length us, event | category | flops | bytes accessed | tf_op | source)
XLA Modules:
  0.0 856.6 jit_solution(4533102890034049058)
XLA Ops:
  8.9 4.4 collective-permute-start
  14.6 9.3 %collective-permute-done = bf16[1,1,64,2048]{2,3,1,0:T(8,128)(2,1)S(1)} collective-permute-done((bf16[1,1,64,2048]{2,3,1,0:T(8,128)(2,1)S(1)}, bf16[1,1,64,2048]{2,3,1,0:T(8,128)(2,1)S(1)}, u32[]{:S(2)}, u32[]{:S(2)}) %collective-permute-start) | collective-permute-done | bytes 262176 | tf_op jit(solution)/shard_map/ppermute | solution.py:16
  23.8 4.2 collective-permute-done.1
  31.7 6.8 copy.179
  40.0 11.3 %fusion.16 = (f32[2,64,8,9,64]{4,2,3,1,0:T(8,128)S(1)}, f32[2,64,8,9,64]{4,2,3,1,0:T(8,128)}) fusion(f32[64]{0:T(128)S(1)} %copy-done.8, pred[8,9]{0,1:T(8,128)(4,1)S(1)} %copy-done.11, bf16[3,3,3,32,64]{4,3,2,1,0:T(8,128)(2,1)S(1)} %copy-done.6, bf16[4,64,1,7,2,32]{5,3,4,1,0,2:T(8,128)(2,1)S(1)} %slice.27, bf16[4,64,1,8,9,32]{5,3,4,1,0,2:T(8,128)(2,1)} %copy.179), kind=kOutput, calls=%fused_computation.18 | convolution fusion | flops 1018822656 | bytes 6238536 | tf_op jit(solution)/shard_map/conv_general_dilated | solution.py:26
  54.2 3.3 reduce_sum.36
  58.0 4.2 collective-permute-start.2
  64.1 5.4 copy.198
  69.5 13.0 %copy.205 = bf16[1,4,64,64,32]{4,0,3,2,1:T(2,128)(2,1)} copy(bf16[1,4,64,64,32]{2,4,3,1,0:T(8,128)(2,1)S(1)} %bitcast.106) | data formatting | bytes 2097152 | tf_op jit(solution)/shard_map/reshape | solution.py:74
  90.5 4.9 collective-permute-start.4
  96.9 8.1 fusion.56
  104.9 82.1 %psum.47 = f32[128]{0:T(128)} all-reduce(f32[128]{0:T(128)S(1)} %get-tuple-element.35), channel_id=1, replica_groups=mesh['dp'=16,'space'=16] {'dp','space'}, use_global_device_ids=true, to_apply=%region_9.10 | all-reduce | flops 128 | bytes 1024 | tf_op jit(solution)/shard_map/psum | solution.py:90
  195.5 83.7 %fusion.18 = f32[3,3,3,32,64]{4,3,2,1,0:T(8,128)} fusion(bf16[1,4,64,64,32]{4,0,3,2,1:T(2,128)(2,1)S(1)} %bitcast.116, bf16[1,2,64,64,64]{4,3,2,1,0:T(8,128)(2,1)S(1)} %bitcast.108), kind=kOutput, calls=%fused_computation.25 | convolution fusion | flops 887193600 | bytes 2318336 | tf_op jit(solution)/shard_map/conv_general_dilated | solution.py:37
  284.8 4.5 collective-permute-start.6
  290.5 2.8 convert_reduce_fusion
  293.3 30.4 %psum.44 = f32[64]{0:T(128)S(1)} all-reduce(f32[64]{0:T(128)S(1)} %convert_reduce_fusion), channel_id=1, replica_groups=mesh['dp'=16,'space'=16] {'space'}, use_global_device_ids=true, to_apply=%region_5.0 | all-reduce | flops 64 | bytes 512 | tf_op jit(solution)/shard_map/psum | solution.py:106
  323.7 39.1 %psum.45 = f32[64]{0:T(128)S(1)} all-reduce(f32[64]{0:T(128)S(1)} %psum.44), channel_id=1, replica_groups=mesh['dp'=16,'space'=16] {'dp'}, use_global_device_ids=true, to_apply=%region_6.0 | all-reduce | flops 64 | bytes 512 | tf_op jit(solution)/shard_map/psum | solution.py:106
  363.4 36.3 %all-reduce.4.cloned.1.call-done = f32[3,3,3,32,64]{4,3,2,1,0:T(8,128)} async-done(((f32[3,3,3,32,64]{4,3,2,1,0:T(8,128)}), f32[3,3,3,32,64]{4,3,2,1,0:T(8,128)}) %all-reduce.4.cloned.1.call-update) | async-done | bytes 221200 | tf_op jit(solution)/shard_map/psum | solution.py:106
  399.7 268.8 %all-reduce.8.cloned.1.call-done = f32[3,3,3,64,128]{4,3,2,1,0:T(8,128)} async-done(((f32[3,3,3,64,128]{4,3,2,1,0:T(8,128)}), f32[3,3,3,64,128]{4,3,2,1,0:T(8,128)}) %all-reduce.8.cloned.1.call-update) | async-done | bytes 884752 | tf_op jit(solution)/shard_map/psum | solution.py:90
  670.6 140.2 %all-reduce.6.cloned.1.call-done = f32[3,3,3,32,64]{4,3,2,1,0:T(8,128)} async-done(((f32[3,3,3,32,64]{4,3,2,1,0:T(8,128)}), f32[3,3,3,32,64]{4,3,2,1,0:T(8,128)}) %all-reduce.6.cloned.1.call-update) | async-done | bytes 221200 | tf_op jit(solution)/shard_map/psum | solution.py:106
  812.7 2.8 concatenate.34
  823.8 3.0 copy.203
  827.1 18.0 %fusion.4 = bf16[2,64,8,9,32]{4,2,3,1,0:T(8,128)(2,1)} fusion(bf16[3,3,3,32,64]{4,3,2,1,0:T(8,128)(2,1)S(1)} %copy-done.7, bf16[4,64,1,7,2,64]{5,3,4,1,0,2:T(8,128)(2,1)S(1)} %slice.36, bf16[4,64,1,8,9,64]{5,3,4,1,0,2:T(8,128)(2,1)S(1)} %copy.203), kind=kOutput, calls=%fused_computation.6 | convolution fusion | flops 1017249792 | bytes 3518464 | tf_op jit(solution)/shard_map/conv_general_dilated | solution.py:48
  845.2 3.2 copy.204
  (105 shorter events, 52.4 us)
Async XLA Ops:
  7.2 81.2 %copy-start = (bf16[3,3,3,64,128]{4,3,2,1,0:T(8,128)(2,1)S(1)}, bf16[3,3,3,64,128]{4,3,2,1,0:T(8,128)(2,1)}, u32[]{:S(2)}) copy-start(bf16[3,3,3,64,128]{4,3,2,1,0:T(8,128)(2,1)} %param.9) | copy-start | bytes 1327108
  7.2 392.5 %all-reduce.4.cloned.1.call-start = ((), (), s32[]{:S(2)}) async-start(), calls=%async_computation | async-start | bytes 884736 | tf_op jit(solution)/shard_map/psum | solution.py:106
  8.8 15.0 %copy-start.3 = (bf16[1,2,64,2048]{2,3,1,0:T(8,128)(2,1)}, bf16[1,2,64,2048]{2,3,1,0:T(8,128)(2,1)S(1)}, u32[]{:S(2)}) copy-start(bf16[1,2,64,2048]{2,3,1,0:T(8,128)(2,1)S(1)} %copy.175) | copy-start | bytes 1572868
  8.9 15.0 %collective-permute-start = (bf16[1,1,64,2048]{2,3,1,0:T(8,128)(2,1)S(1)}, bf16[1,1,64,2048]{2,3,1,0:T(8,128)(2,1)S(1)}, u32[]{:S(2)}, u32[]{:S(2)}) collective-permute-start(bf16[1,1,64,2048]{2,3,1,0:T(8,128)(2,1)S(1)} %get-tuple-element.43), channel_id=1, source_target_pairs={{0,1},{1,2},{2,3},{3,4},{4,5},{5,6},{6,7},{7,8},{8,9},{9,10},{10,1... | collective-permute-start | bytes 786440 | tf_op jit(solution)/shard_map/ppermute | solution.py:16
  13.3 14.7 %collective-permute-start.1 = (bf16[1,1,64,2048]{2,3,1,0:T(8,128)(2,1)S(1)}, bf16[1,1,64,2048]{2,3,1,0:T(8,128)(2,1)S(1)}, u32[]{:S(2)}, u32[]{:S(2)}) collective-permute-start(bf16[1,1,64,2048]{2,3,1,0:T(8,128)(2,1)S(1)} %get-tuple-element.44), channel_id=1, source_target_pairs={{1,0},{2,1},{3,2},{4,3},{5,4},{6,5},{7,6},{8,7},{9,8},{10,9},{11,1... | collective-permute-start | bytes 786440 | tf_op jit(solution)/shard_map/ppermute | solution.py:18
  31.7 8.3 copy-start.6
  31.7 8.3 copy-start.8
  31.7 8.3 copy-start.11
  52.2 10.0 %copy-start.4 = (bf16[1,1,32,4096]{3,2,1,0:T(8,128)(2,1)S(1)}, bf16[1,1,32,4096]{3,2,1,0:T(8,128)(2,1)}, u32[]{:S(2)}) copy-start(bf16[1,1,32,4096]{3,2,1,0:T(8,128)(2,1)} %param.11) | copy-start | bytes 786436
  58.0 24.5 %collective-permute-start.2 = (bf16[1,1,32,2048]{3,2,1,0:T(8,128)(2,1)S(1)}, bf16[1,1,32,2048]{3,2,1,0:T(8,128)(2,1)}, u32[]{:S(2)}, u32[]{:S(2)}) collective-permute-start(bf16[1,1,32,2048]{3,2,1,0:T(8,128)(2,1)S(1)} %convert_element_type.57), channel_id=1, source_target_pairs={{0,1},{1,2},{2,3},{3,4},{4,5},{5,6},{6,7},{7,8},{8,9},{9,10},{10,1... | collective-permute-start | bytes 393224 | tf_op jit(solution)/shard_map/ppermute | solution.py:16
  62.3 22.6 %collective-permute-start.3 = (bf16[1,1,32,2048]{3,2,1,0:T(8,128)(2,1)S(1)}, bf16[1,1,32,2048]{3,2,1,0:T(8,128)(2,1)}, u32[]{:S(2)}, u32[]{:S(2)}) collective-permute-start(bf16[1,1,32,2048]{3,2,1,0:T(8,128)(2,1)S(1)} %convert_element_type.57), channel_id=1, source_target_pairs={{1,0},{2,1},{3,2},{4,3},{5,4},{6,5},{7,6},{8,7},{9,8},{10,9},{11,1... | collective-permute-start | bytes 393224 | tf_op jit(solution)/shard_map/ppermute | solution.py:18
  90.5 96.5 %collective-permute-start.4 = (bf16[1,1,32,4096]{3,2,1,0:T(8,128)(2,1)S(1)}, bf16[1,1,32,4096]{3,2,1,0:T(8,128)(2,1)S(1)}, u32[]{:S(2)}, u32[]{:S(2)}) collective-permute-start(bf16[1,1,32,4096]{3,2,1,0:T(8,128)(2,1)S(1)} %reshape.106), channel_id=1, source_target_pairs={{0,1},{1,2},{2,3},{3,4},{4,5},{5,6},{6,7},{7,8},{8,9},{9,10},{10,1... | collective-permute-start | bytes 786440 | tf_op jit(solution)/shard_map/ppermute | solution.py:16
  95.4 91.7 %collective-permute-start.5 = (bf16[1,1,32,4096]{3,2,1,0:T(8,128)(2,1)S(1)}, bf16[1,1,32,4096]{3,2,1,0:T(8,128)(2,1)S(1)}, u32[]{:S(2)}, u32[]{:S(2)}) collective-permute-start(bf16[1,1,32,4096]{3,2,1,0:T(8,128)(2,1)S(1)} %reshape.106), channel_id=1, source_target_pairs={{1,0},{2,1},{3,2},{4,3},{5,4},{6,5},{7,6},{8,7},{9,8},{10,9},{11,1... | collective-permute-start | bytes 786440 | tf_op jit(solution)/shard_map/ppermute | solution.py:18
  188.0 3.8 slice-start
  188.2 3.7 slice-start.1
  190.7 4.8 slice-start.2
  191.9 3.6 slice-start.3
  195.5 83.8 %copy-start.10 = (f32[128]{0:T(128)S(1)}, f32[128]{0:T(128)}, u32[]{:S(2)}) copy-start(f32[128]{0:T(128)} %psum.47) | copy-start | bytes 1540
  279.2 389.2 %all-reduce.8.cloned.1.call-start = ((), (), s32[]{:S(2)}) async-start(), calls=%async_computation.2 | async-start | bytes 1769472 | tf_op jit(solution)/shard_map/psum | solution.py:90
  280.0 530.9 %all-reduce.6.cloned.1.call-start = ((), (), s32[]{:S(2)}) async-start(), calls=%async_computation.1 | async-start | bytes 884736 | tf_op jit(solution)/shard_map/psum | solution.py:106
  284.8 527.9 %collective-permute-start.6 = (bf16[1,1,64,4096]{3,2,1,0:T(8,128)(2,1)}, bf16[1,1,64,4096]{3,2,1,0:T(8,128)(2,1)}, u32[]{:S(2)}, u32[]{:S(2)}) collective-permute-start(bf16[1,1,64,4096]{3,2,1,0:T(8,128)(2,1)} %get-tuple-element.41), channel_id=1, source_target_pairs={{0,1},{1,2},{2,3},{3,4},{4,5},{5,6},{6,7},{7,8},{8,9},{9,10},{10,1... | collective-permute-start | bytes 1572872 | tf_op jit(solution)/shard_map/ppermute | solution.py:16
  289.2 526.2 %collective-permute-start.7 = (bf16[1,1,64,4096]{3,2,1,0:T(8,128)(2,1)}, bf16[1,1,64,4096]{3,2,1,0:T(8,128)(2,1)S(1)}, u32[]{:S(2)}, u32[]{:S(2)}) collective-permute-start(bf16[1,1,64,4096]{3,2,1,0:T(8,128)(2,1)} %get-tuple-element.42), channel_id=1, source_target_pairs={{1,0},{2,1},{3,2},{4,3},{5,4},{6,5},{7,6},{8,7},{9,8},{10,9},{11,1... | collective-permute-start | bytes 1572872 | tf_op jit(solution)/shard_map/ppermute | solution.py:18
  827.1 21.2 %copy-start.5 = (pred[8,9]{1,0:T(8,128)(4,1)S(1)}, pred[8,9]{1,0:T(8,128)(4,1)}, u32[]{:S(2)}) copy-start(pred[8,9]{1,0:T(8,128)(4,1)} %constant.34) | copy-start | bytes 220
  827.1 22.8 %copy-start.1 = (bf16[3,3,3,64,128]{4,3,2,1,0:T(8,128)(2,1)S(1)}, bf16[3,3,3,64,128]{4,3,2,1,0:T(8,128)(2,1)}, u32[]{:S(2)}) copy-start(bf16[3,3,3,64,128]{4,3,2,1,0:T(8,128)(2,1)} %param.9) | copy-start | bytes 1327108
  (4 other events, 11.7 us)
Sparse Core Ops, SparseCore 0:
  279.3 120.2 all-reduce.3
  405.7 262.6 all-reduce.7
  671.1 139.7 all-reduce.5
